TPU v7x, 32 devices: a whole 2x2x4 slice. The times are simulated.
32 devices in a mesh: rows: 8 (over y, x, core), grp: 4 (over z).
Axes of the slice: x: 2, y: 2, z: 4, core: 2. Of those that a mesh axis runs over, the one named last changes fastest.
Arguments:
- momenta: float32 [128, 4, 24576], P('rows', 'grp'), may hold values from -6 to 6
Outputs:
- basis_out: float32 [128, 4, 24576], P(None, 'grp', 'rows')
- factor: float32 [128, 128], replicated
All inputs are finite; a program needn't handle non-finite values.
Results may differ from a plain program's by a relative error of at most 0.0003.
Values sent between devices are 32-bit elements; how exact they have to be, the bound alone decides.
No kernel may reach another device: no remote copies, remote signals or barrier semaphores. Data moves between devices by JAX's collectives and lax.ppermute only.
A program may use at most 192 MiB of HBM per device.

v0:
```python
import math
import jax
import jax.numpy as jnp
from jax import lax
from jax.sharding import PartitionSpec as P


def cross_products(left_mat, right_mat):
    return lax.dot_general(
        left_mat,
        right_mat,
        (((1,), (1,)), ((), ())),
        precision=lax.Precision.HIGHEST,
        preferred_element_type=jnp.float32,
    )


def upper_of(gram_matrix):
    return jnp.linalg.cholesky(gram_matrix).T


def lower_solve(lower_factor, right_hand):
    return lax.linalg.triangular_solve(lower_factor, right_hand, left_side=True, lower=True)


def on_device(momenta):
    voxel_panel = lax.all_to_all(momenta, "rows", split_axis=2, concat_axis=0, tiled=True)
    subject_rows = voxel_panel[:, 0, :]
    all_rows = subject_rows.shape[1] * lax.axis_size("rows") * lax.axis_size("grp")
    gram_matrix = cross_products(subject_rows, subject_rows)
    summed = lax.psum(gram_matrix, ("rows", "grp"))
    upper_factor = upper_of(summed)
    lower_factor = upper_factor.T
    ortho_t = lower_solve(lower_factor, subject_rows)
    scale = math.sqrt(all_rows)
    basis_out = (ortho_t * scale)[:, None, :]
    return (basis_out, upper_factor / scale)


def solution(mesh):
    return jax.shard_map(
        on_device,
        mesh=mesh,
        in_specs=(P("rows", "grp", None),),
        out_specs=(P(None, "grp", "rows"), P()),
        check_vma=False,
    )
```

profile of v0, /device:TPU:1, one launch (start us, length us, event | category | flops | bytes accessed | tf_op | source)
XLA Modules:
  0.0 378.4 jit_solution(2650943112555666837)
XLA Ops:
  7.2 0.0 all-reduce.2.cloned.1.call-start
  7.2 22.8 %copy.23 = f32[16,1,24576]{0,1,2:T(1,128)} copy(f32[16,1,24576]{2,1,0:T(1,128)} %param.1) | data formatting | bytes 3145728 | tf_op args[0]
  30.0 0.5 broadcast.50
  30.6 110.5 %reduce.6 = f32[24576,16]{1,0:T(8,128)} reduce(f32[24576,1,16]{2,1,0:T(1,128)} %bitcast.22, f32[]{:T(128)} %broadcast.50), dimensions={1}, to_apply=%bitcast.16.reduce_sub_computation | reduce | bytes 3145732
  141.1 8.9 %reshape.14 = f32[8,1,49152]{2,1,0:T(1,128)S(1)} reshape(f32[24576,16]{1,0:T(8,128)} %reduce.6) | data formatting | bytes 3145728
  149.9 24.7 %all_to_all.15 = f32[8,1,49152]{2,1,0:T(1,128)S(1)} all-to-all(f32[8,1,49152]{2,1,0:T(1,128)S(1)} %reshape.14), channel_id=1, replica_groups=mesh['rows'=8,'grp'=4] {'rows'}, dimensions={0} | all-to-all | bytes 3145728 | tf_op jit(solution)/shard_map/all_to_all | solution.py:27
  174.6 4.4 %reduce.7 = f32[8,49152]{1,0:T(8,128)S(1)} reduce(f32[8,1,49152]{2,1,0:T(1,128)S(1)} %all_to_all.15, f32[]{:T(128)} %broadcast.50), dimensions={1}, to_apply=%all_to_all.11.reduce_sub_computation | reduce | bytes 3145732 | tf_op jit(solution)/shard_map/all_to_all | solution.py:27
  179.0 30.7 %reshape.15 = f32[24576,1,16]{2,1,0:T(1,128)} reshape(f32[8,49152]{1,0:T(8,128)S(1)} %reduce.7) | data formatting | bytes 3145728
  209.8 7.6 %copy.31 = f32[16,1,8,3072]{3,2,0,1:T(8,128)S(1)} copy(f32[16,1,8,3072]{0,3,2,1:T(8,128)} %bitcast.21) | data formatting | bytes 3145728 | tf_op jit(solution)/shard_map/all_to_all | solution.py:27
  217.4 0.9 copy.25
  218.3 2.0 fusion.3
  220.4 0.0 all-reduce.2.cloned.1.call-update
  220.4 121.3 %all-reduce.2.cloned.1.call-done = f32[128,128]{0,1:T(8,128)} async-done(((f32[128,128]{0,1:T(8,128)}), f32[128,128]{0,1:T(8,128)}) %all-reduce.2.cloned.1.call-update) | async-done | bytes 65552 | tf_op jit(solution)/shard_map/psum | solution.py:31
  341.7 0.9 copy.27
  342.7 0.9 fusion.2
  343.5 11.7 %cholesky.16 = f32[128,128]{1,0:T(8,128)S(1)} custom-call(f32[128,128]{1,0:T(8,128)S(1)} %fusion.2), custom_call_target="Cholesky" | custom-call | tf_op jit(solution)/shard_map/jit(cholesky)/cholesky | solution.py:19
  355.3 0.6 compare_reduce_fusion
  355.9 0.7 multiply_bitcast_fusion
  356.6 0.7 copy.29
  357.3 9.8 %custom-call.6 = f32[1,128,128]{1,2,0:T(8,128)S(1)} custom-call(f32[1,128,128]{2,1,0:T(8,128)S(1)} %get-tuple-element.13), custom_call_target="InvertDiagBlocksLowerTriangular" | custom-call | tf_op jit(solution)/shard_map/triangular_solve | solution.py:23
  367.1 1.5 fusion
  368.6 2.8 copy.28
  (1 shorter events, 0.0 us)
Async XLA Ops:
  7.2 334.6 %all-reduce.2.cloned.1.call-start = ((), (), s32[]{:S(2)}) async-start(), calls=%async_computation.1 | async-start | bytes 131072 | tf_op jit(solution)/shard_map/psum | solution.py:31
Sparse Core Ops, SparseCore 0:
  220.5 121.1 all-reduce.1
where the time goes:
time: 385 us; the launch traced here: 378 us
  other arithmetic  139 us (36%)
  waiting for transfers between devices  121 us (31%)
  local copies, waits for them, and re-layouts  75.9 us (20%)
  blocking collectives  24.7 us (6%)
  between operations  14.3 us (4%)
    psum x1, waiting for transfers between devices, on_device(): summed = lax.psum(gram_matrix, ('rows', 'grp'))  121 us
    unnamed x1, other arithmetic  110 us
    unnamed x6, local copies, waits for them, and re-layouts  66.4 us
    all_to_all x1, blocking collectives, on_device(): lax.all_to_all(momenta, 'rows', split_axis=2, concat_axis=0, tiled=True)  24.7 us
    another operation x3, other arithmetic, upper_of(): return jnp.linalg.cholesky(gram_matrix).T  12.4 us
    another operation x1, other arithmetic, lower_solve(): lax.linalg.triangular_solve(lower_factor, right_hand, left_side=True, low...  9.81 us
    all_to_all x2, local copies, waits for them, and re-layouts, on_device(): lax.all_to_all(momenta, 'rows', split_axis=2, concat_axis=0, tiled=True)  8.56 us
  transfers between devices with their start and end apart: 1, of which 1 were waited for; matrix products, arithmetic and copies ran while one was open for 0% of the time, Pallas kernels for 0%

commit v1 on v0

--- a/solution.py
+++ b/solution.py
@@ -24,7 +24,9 @@
 
 
 def on_device(momenta):
-    voxel_panel = lax.all_to_all(momenta, "rows", split_axis=2, concat_axis=0, tiled=True)
+    pieces = jnp.split(momenta, lax.axis_size("rows"), axis=2)
+    incoming = lax.all_to_all(jnp.stack(pieces), "rows", 0, 0)
+    voxel_panel = jnp.concatenate(incoming, axis=0)
     subject_rows = voxel_panel[:, 0, :]
     all_rows = subject_rows.shape[1] * lax.axis_size("rows") * lax.axis_size("grp")
     gram_matrix = cross_products(subject_rows, subject_rows)

time: 385 us -> 200 us (0.52); the launches traced: 378 us -> 200 us
  other arithmetic: 139 us -> 23.7 us
  local copies, waits for them, and re-layouts: 75.9 us -> 12.3 us
    unnamed x1 -> x0, other arithmetic: 110 us -> none
    unnamed x6 -> x10, local copies, waits for them, and re-layouts: 66.4 us -> 10.5 us
    all_to_all x2 -> x0, local copies, waits for them, and re-layouts: 8.56 us -> none  [on_device(): lax.all_to_all(momenta, 'rows', split_axis=2, concat_axis=0, tiled=True)]
    all_to_all x1 -> x0, other arithmetic: 4.38 us -> none  [on_device(): lax.all_to_all(momenta, 'rows', split_axis=2, concat_axis=0, tiled=True)]
where the time goes in v1:
time: 200 us
  waiting for transfers between devices  121 us (60%)
  blocking collectives  24.7 us (12%)
  other arithmetic  23.7 us (12%)
  between operations  14.1 us (7%)
  local copies, waits for them, and re-layouts  12.3 us (6%)
  matrix products  3.51 us (2%)
    psum x1, waiting for transfers between devices, on_device(): summed = lax.psum(gram_matrix, ('rows', 'grp'))  121 us
    all_to_all x1, blocking collectives, on_device(): incoming = lax.all_to_all(jnp.stack(pieces), 'rows', 0, 0)  24.7 us
    another operation x3, other arithmetic, upper_of(): return jnp.linalg.cholesky(gram_matrix).T  12.4 us
    unnamed x10, local copies, waits for them, and re-layouts  10.5 us
    another operation x1, other arithmetic, lower_solve(): lax.linalg.triangular_solve(lower_factor, right_hand, left_side=True, low...  9.81 us
  transfers between devices with their start and end apart: 1, of which 1 were waited for; matrix products, arithmetic and copies ran while one was open for 0% of the time, Pallas kernels for 0%

profile of v1, /device:TPU:1, one launch (start us, length us, event | category | flops | bytes accessed | tf_op | source)
XLA Modules:
  0.0 199.8 jit_solution(14320720991083701514)
XLA Ops:
  7.2 0.0 all-reduce.2.cloned.1.call-start
  7.2 0.9 bitcast_dynamic-update-slice_fusion.7
  8.2 1.0 bitcast_dynamic-update-slice_fusion.6
  9.1 1.0 bitcast_dynamic-update-slice_fusion.5
  10.1 1.0 bitcast_dynamic-update-slice_fusion.4
  11.0 1.0 bitcast_dynamic-update-slice_fusion.3
  12.0 1.0 bitcast_dynamic-update-slice_fusion.2
  13.0 1.0 bitcast_dynamic-update-slice_fusion.1
  13.9 1.0 bitcast_dynamic-update-slice_fusion
  14.9 24.7 %all_to_all.5 = f32[8,16,1,3072]{3,2,1,0:T(1,128)S(1)} all-to-all(f32[8,16,1,3072]{3,2,1,0:T(1,128)S(1)} %bitcast_dynamic-update-slice_fusion), channel_id=1, replica_groups=mesh['rows'=8,'grp'=4] {'rows'}, dimensions={0} | all-to-all | bytes 3145728 | tf_op jit(solution)/shard_map/all_to_all | solution.py:28
  39.6 0.3 copy.8
  39.9 2.0 %fusion.3 = f32[128,128]{0,1:T(8,128)} fusion(f32[128,3072]{1,0:T(8,128)S(1)} %bitcast.33), kind=kOutput, calls=%fused_computation.20 | convolution fusion | flops 603979776 | bytes 1638400 | tf_op jit(solution)/shard_map/dot_general | solution.py:9
  41.9 0.0 all-reduce.2.cloned.1.call-update
  41.9 121.3 %all-reduce.2.cloned.1.call-done = f32[128,128]{0,1:T(8,128)} async-done(((f32[128,128]{0,1:T(8,128)}), f32[128,128]{0,1:T(8,128)}) %all-reduce.2.cloned.1.call-update) | async-done | bytes 65552 | tf_op jit(solution)/shard_map/psum | solution.py:33
  163.3 0.9 copy.4
  164.2 0.9 fusion.2
  165.1 11.7 %cholesky.16 = f32[128,128]{1,0:T(8,128)S(1)} custom-call(f32[128,128]{1,0:T(8,128)S(1)} %fusion.2), custom_call_target="Cholesky" | custom-call | tf_op jit(solution)/shard_map/jit(cholesky)/cholesky | solution.py:19
  176.8 0.6 compare_reduce_fusion
  177.5 0.7 multiply_bitcast_fusion
  178.1 0.7 copy.6
  178.9 9.8 %custom-call.6 = f32[1,128,128]{1,2,0:T(8,128)S(1)} custom-call(f32[1,128,128]{2,1,0:T(8,128)S(1)} %get-tuple-element.5), custom_call_target="InvertDiagBlocksLowerTriangular" | custom-call | tf_op jit(solution)/shard_map/triangular_solve | solution.py:23
  188.7 1.5 fusion
  190.2 2.8 %copy.5 = f32[128,1,3072]{2,1,0:T(1,128)} copy(f32[128,1,3072]{2,0,1:T(8,128)S(1)} %fusion) | data formatting | bytes 3145728
  (1 shorter events, 0.0 us)
Async XLA Ops:
  7.2 156.1 %all-reduce.2.cloned.1.call-start = ((), (), s32[]{:S(2)}) async-start(), calls=%async_computation.1 | async-start | bytes 131072 | tf_op jit(solution)/shard_map/psum | solution.py:33
Sparse Core Ops, SparseCore 0:
  42.1 121.1 all-reduce.1
